TPU v7x, 32 devices: a whole 2x2x4 slice. The times are simulated.
32 devices in a mesh: slab: 8 (over y, x, core), tm: 4 (over z).
Axes of the slice: x: 2, y: 2, z: 4, core: 2. Of those that a mesh axis runs over, the one named last changes fastest.
Arguments:
- field: float32 [2, 128, 256, 512], P(None, 'slab', None, 'tm'), may hold values from -110 to 110
Outputs:
- evolved: float32 [2, 128, 256, 512], P(None, 'slab', None, 'tm')
All inputs are finite; a program needn't handle non-finite values.
Results may differ from a plain program's by a relative error of at most 0.000098.
Values sent between devices are 32-bit elements; how exact they have to be, the bound alone decides.
A program may use at most 128 MiB of HBM per device.

v0:
```python
import functools
import math

import ml_dtypes
import numpy as np

import jax
import jax.numpy as jnp
from jax import lax
from jax.experimental import pallas as pl
from jax.experimental.pallas import tpu as pltpu
from jax.sharding import PartitionSpec as P

TWO_PI = 2.0 * math.pi
DIFFRACT = 4.0
DISPERSE = 3.0
KERR = 0.05
WELL = 1.5
EPSILON = 1e-06
AXES = ("slab", "tm")
PIECE = 1
LANES = 128
WIDE = 256
MESH = pl.DeviceIdType.MESH


def matrix(length, strength):
    steps = np.arange(length)
    signed = np.where(2 * steps < length, steps, steps - length)
    phase = np.exp(1j * strength * (TWO_PI * signed / length) ** 2)
    response = np.fft.ifft(phase)
    return response[(steps[:, None] - steps[None, :]) % length]


def propagator(length, strength):
    whole = matrix(length, strength)
    real = jnp.asarray(whole.real.astype(np.float32))
    imag = jnp.asarray(whole.imag.astype(np.float32))
    upper = jnp.stack([real, -imag], axis=1)
    lower = jnp.stack([imag, real], axis=1)
    return jnp.stack([upper, lower])


def halves(table):
    table = table.astype(np.float32)
    high = table.astype(ml_dtypes.bfloat16)
    low = (table - high.astype(np.float32)).astype(ml_dtypes.bfloat16)
    return high, low


def blocks(whole):
    return np.block([[whole.real, -whole.imag], [whole.imag, whole.real]])


def apply(form, table, value):
    return jnp.einsum(form, table, value, precision=lax.Precision.HIGH)


def place(index, length):
    return (index.astype(jnp.float32) - (length - 1) / 2.0) / (length / 2.0)


def kick(real, imag, scale, well_depth):
    real = real * scale
    imag = imag * scale
    angle = KERR * (real * real + imag * imag) - well_depth
    turn_c = jnp.cos(angle)
    turn_s = jnp.sin(angle)
    return real * turn_c - imag * turn_s, real * turn_s + imag * turn_c


def split(value):
    high = value.astype(jnp.bfloat16)
    low = (value - high.astype(jnp.float32)).astype(jnp.bfloat16)
    return high, low


def dot(left, right):
    return jnp.dot(left, right, preferred_element_type=jnp.float32)


def left_table(table, high, low):
    n = table.shape[0] // 2
    both = dot(table, high)
    return both[:n] + both[n:] + dot(table[:n], low)


def step_kernel(
    dims,
    field_ref,
    fwd_ref,
    across_ref,
    time_ref,
    back_ref,
    out_ref,
    fld,
    fh,
    fl,
    fwd,
    across,
    wt,
    back,
    turn,
    send,
    recv,
    xh,
    xl,
    ysp,
    ksp,
    hsend,
    home,
    acc,
    pw_send,
    pw_recv,
    load_sem,
    table_sem,
    out_sem,
    send_sem,
    recv_sem,
    hsend_sem,
    home_sem,
    pw_sem,
):
    slabs, times, rows, ny, cols, piece, chunks = dims
    devices = slabs * times
    nx, nt = slabs * rows, times * cols
    group = devices * piece
    blk = piece * 2 * rows
    pitch = turn.shape[0] // rows
    pairs = rows // 2
    s = lax.axis_index("slab")
    m = lax.axis_index("tm")
    me = s * times + m

    def field_copy(xp):
        part = (slice(None), pl.ds(2 * xp, 2))
        return pltpu.make_async_copy(field_ref.at[part], fld.at[part], load_sem.at[xp])

    for xp in range(pairs):
        field_copy(xp).start()
    tables = [
        pltpu.make_async_copy(a, b, table_sem.at[i])
        for i, (a, b) in enumerate(
            [(fwd_ref, fwd), (across_ref, across), (time_ref, wt), (back_ref, back)]
        )
    ]
    for copy in tables:
        copy.start()

    barrier = pltpu.get_barrier_semaphore()

    def greet(k, carry):
        peer = (me + k) % devices
        pl.semaphore_signal(
            barrier, inc=1, device_id=(peer // times, peer % times), device_id_type=MESH
        )
        return carry

    lax.fori_loop(1, devices, greet, 0)

    def prepare(xp, total):
        field_copy(xp).wait()
        for q in range(2):
            value = jnp.concatenate([fld[q, 2 * xp], fld[q, 2 * xp + 1]], axis=1)
            high, low = split(value)
            fh[xp, pl.ds(q * ny, ny), :] = high
            fl[xp, pl.ds(q * ny, ny), :] = low
            total = total + jnp.sum((value * value).reshape(ny // 8, 8, 2 * cols), axis=0)
        return total

    total = lax.fori_loop(0, pairs, prepare, jnp.zeros((8, 2 * cols), jnp.float32))
    total = total[:, :cols] + total[:, cols:]
    pw_send[...] = total
    pw_recv[me] = total

    half = times // 2
    side = m // half
    order = []
    for i in range(half):
        order.append([(1 - side) * half + (m + i) % half, False])
    for i in range(1, half):
        order.append([side * half + (m + i) % half, False])
    order.append([m, True])

    def to_all(make):
        for there, own in order:
            for k in range(slabs):
                if own and k == 0:
                    continue
                make((s + k) % slabs, there)

    def forward_copy(c, ds, dm):
        return pltpu.make_async_remote_copy(
            src_ref=send.at[c, pl.ds((ds * times + dm) * blk, blk)],
            dst_ref=recv.at[c, pl.ds(me * blk, blk)],
            send_sem=send_sem.at[c],
            recv_sem=recv_sem.at[c],
            device_id=(ds, dm),
            device_id_type=MESH,
        )

    def home_copy(c, ds, dm):
        return pltpu.make_async_remote_copy(
            src_ref=hsend.at[c, pl.ds((ds * times + dm) * blk, blk)],
            dst_ref=home.at[c, pl.ds(me * blk, blk)],
            send_sem=hsend_sem.at[c],
            recv_sem=home_sem.at[c],
            device_id=(ds, dm),
            device_id_type=MESH,
        )

    def power_copy(ds, dm):
        return pltpu.make_async_remote_copy(
            src_ref=pw_send,
            dst_ref=pw_recv.at[me],
            send_sem=pw_sem.at[0],
            recv_sem=pw_sem.at[1],
            device_id=(ds, dm),
            device_id_type=MESH,
        )

    def whole(src, dst, first, second):
        return pltpu.make_async_remote_copy(
            src_ref=src,
            dst_ref=dst,
            send_sem=first,
            recv_sem=second,
            device_id=(s, m),
            device_id_type=MESH,
        )

    others = pl.ds(0, (devices - 1) * blk)

    def spread(c):
        def along_y(xp, carry):
            result = left_table(fwd[c], fh[xp], fl[xp])
            turn[pl.ds(2 * xp * pitch, 2 * group), :] = result[:, :cols]
            turn[pl.ds((2 * xp + 1) * pitch, 2 * group), :] = result[:, cols:]
            return carry

        lax.fori_loop(0, pairs, along_y, 0)
        for r in range(group):
            for q in range(2):
                send[c, pl.ds((r * 2 + q) * rows, rows), :] = turn[
                    pl.ds(q * group + r, rows, stride=pitch), :
                ]
        for j in range(piece):
            for q in range(2):
                recv[c, pl.ds(me * blk + (j * 2 + q) * rows, rows), :] = turn[
                    pl.ds(q * group + me * piece + j, rows, stride=pitch), :
                ]

    tables[0].wait()
    spread(0)
    pl.semaphore_wait(barrier, devices - 1)
    to_all(lambda ds, dm: forward_copy(0, ds, dm).start())
    to_all(lambda ds, dm: power_copy(ds, dm).start())

    def rest(c, carry):
        spread(c)
        to_all(lambda ds, dm: forward_copy(c, ds, dm).start())
        return carry

    lax.fori_loop(1, chunks, rest, 0)

    for copy in tables[1:]:
        copy.wait()
    whole(pw_recv.at[pl.ds(0, devices - 1)], pw_recv.at[pl.ds(0, devices - 1)], pw_sem.at[0], pw_sem.at[1]).wait_recv()
    power = jnp.sum(jnp.sum(pw_recv[...], axis=0), axis=(0, 1), keepdims=True)
    scale = 1.0 / jnp.sqrt(power / (nx * ny * nt) + EPSILON)
    place_x = place(lax.broadcasted_iota(jnp.int32, (nx, WIDE), 0), nx)
    square_x = place_x * place_x
    tiles = nt // WIDE
    per_tile = WIDE // cols

    def along_t(source, n):
        lanes = pl.ds(n * WIDE, WIDE)
        parts = []
        for part in range(2):
            both = dot(source[...], wt[part, 0, :, lanes])
            parts.append(
                both[: 2 * nx] + both[2 * nx :] + dot(source[: 2 * nx], wt[part, 1, :, lanes])
            )
        gr, gi = parts
        return gr[:nx] - gi[nx:], gi[:nx] + gr[nx:]

    def middle(c, carry):
        whole(recv.at[c, others], recv.at[c, others], send_sem.at[c], recv_sem.at[c]).wait_recv()
        for j in range(piece):
            for a in range(slabs):
                for b in range(times):
                    for q in range(2):
                        got = recv[
                            c, pl.ds((a * times + b) * blk + (j * 2 + q) * rows, rows), :
                        ]
                        high, low = split(got)
                        xh[pl.ds(q * nx + a * rows, rows), pl.ds(b * cols, cols)] = high
                        xl[pl.ds(q * nx + a * rows, rows), pl.ds(b * cols, cols)] = low
            for n in range(tiles):
                lanes = pl.ds(n * WIDE, WIDE)
                value = left_table(across[...], xh[:, lanes], xl[:, lanes])
                high, low = split(value)
                ysp[pl.ds(0, 2 * nx), lanes] = high
                ysp[pl.ds(2 * nx, 2 * nx), lanes] = low
            y = c * group + me * piece + j
            place_y = (y.astype(jnp.float32) - (ny - 1) / 2.0) / (ny / 2.0)
            well_depth = WELL * (square_x + place_y * place_y)
            for n in range(tiles):
                lanes = pl.ds(n * WIDE, WIDE)
                real, imag = along_t(ysp, n)
                real, imag = kick(real, imag, scale, well_depth)
                for q, value in enumerate((real, imag)):
                    high, low = split(value)
                    ksp[pl.ds(q * nx, nx), lanes] = high
                    ksp[pl.ds((2 + q) * nx, nx), lanes] = low
            for n in range(tiles):
                lanes = pl.ds(n * WIDE, WIDE)
                for q, value in enumerate(along_t(ksp, n)):
                    high, low = split(value)
                    xh[pl.ds(q * nx, nx), lanes] = high
                    xl[pl.ds(q * nx, nx), lanes] = low
            for n in range(tiles):
                lanes = pl.ds(n * WIDE, WIDE)
                value = left_table(across[...], xh[:, lanes], xl[:, lanes])
                for q in range(2):
                    for a in range(slabs):
                        for b in range(per_tile):
                            dest = a * times + n * per_tile + b
                            hsend[c, pl.ds(dest * blk + (j * 2 + q) * rows, rows), :] = value[
                                q * nx + a * rows : q * nx + (a + 1) * rows,
                                b * cols : (b + 1) * cols,
                            ]
        home[c, pl.ds(me * blk, blk), :] = hsend[c, pl.ds(me * blk, blk), :]
        to_all(lambda ds, dm: home_copy(c, ds, dm).start())
        return carry

    lax.fori_loop(0, chunks, middle, 0)

    def gather(c, last):
        whole(home.at[c, others], home.at[c, others], hsend_sem.at[c], home_sem.at[c]).wait_recv()

        def along_y(xp, carry):
            sides = []
            for i in range(2):
                sides.append(
                    jnp.concatenate(
                        [
                            home[c, pl.ds(q * rows + 2 * xp + i, group, stride=2 * rows), :]
                            for q in range(2)
                        ],
                        axis=0,
                    )
                )
            high, low = split(jnp.concatenate(sides, axis=1))
            value = left_table(back[c], high, low)
            for q in range(2):
                for i in range(2):
                    part = value[q * ny : (q + 1) * ny, i * cols : (i + 1) * cols]
                    acc[q, 2 * xp + i] = acc[q, 2 * xp + i] + part
            if last:
                out_copy(xp).start()
            return carry

        lax.fori_loop(0, pairs, along_y, 0)

    def out_copy(xp):
        part = (slice(None), pl.ds(2 * xp, 2))
        return pltpu.make_async_copy(acc.at[part], out_ref.at[part], out_sem.at[xp])

    acc[...] = jnp.zeros_like(acc)

    def early(c, carry):
        gather(c, False)
        return carry

    lax.fori_loop(0, chunks - 1, early, 0)
    gather(chunks - 1, True)

    def drain(c, carry):
        whole(send.at[c, others], send.at[c, others], send_sem.at[c], recv_sem.at[c]).wait_send()
        whole(hsend.at[c, others], hsend.at[c, others], hsend_sem.at[c], home_sem.at[c]).wait_send()
        return carry

    lax.fori_loop(0, chunks, drain, 0)
    whole(pw_recv.at[pl.ds(0, devices - 1)], pw_recv.at[pl.ds(0, devices - 1)], pw_sem.at[0], pw_sem.at[1]).wait_send()
    for xp in range(pairs):
        out_copy(xp).wait()


def in_one_kernel(field, slabs, times, piece):
    _, rows, ny, cols = field.shape
    devices = slabs * times
    nx, nt = rows * slabs, cols * times
    group = devices * piece
    chunks = ny // group
    blk = piece * 2 * rows
    pitch = 2 * group + 8
    uy = matrix(ny, -DIFFRACT)
    ux = matrix(nx, -DIFFRACT)
    ut = matrix(nt, DISPERSE)
    full_y = blocks(uy).reshape(2, ny, 2, ny)
    fwd = np.stack(
        [
            np.concatenate(halves(full_y[:, c * group : (c + 1) * group].reshape(2 * group, 2 * ny)))
            for c in range(chunks)
        ]
    )
    back = np.stack(
        [
            np.concatenate(
                halves(full_y[:, :, :, c * group : (c + 1) * group].reshape(2 * ny, 2 * group))
            )
            for c in range(chunks)
        ]
    )
    across = np.concatenate(halves(blocks(ux)))
    time = np.stack([np.stack(halves(ut.real)), np.stack(halves(ut.imag))])
    dims = (slabs, times, rows, ny, cols, piece, chunks)
    f32, bf16 = jnp.float32, jnp.bfloat16
    any_space = pl.BlockSpec(memory_space=pl.ANY)
    dma = pltpu.SemaphoreType.DMA
    return pl.pallas_call(
        functools.partial(step_kernel, dims),
        out_shape=jax.ShapeDtypeStruct(field.shape, f32),
        in_specs=[any_space] * 5,
        out_specs=any_space,
        scratch_shapes=[
            pltpu.VMEM(field.shape, f32),
            pltpu.VMEM((rows // 2, 2 * ny, 2 * cols), bf16),
            pltpu.VMEM((rows // 2, 2 * ny, 2 * cols), bf16),
            pltpu.VMEM(fwd.shape, bf16),
            pltpu.VMEM(across.shape, bf16),
            pltpu.VMEM(time.shape, bf16),
            pltpu.VMEM(back.shape, bf16),
            pltpu.VMEM((rows * pitch, cols), f32),
            pltpu.VMEM((chunks, devices * blk, cols), f32),
            pltpu.VMEM((chunks, devices * blk, cols), f32),
            pltpu.VMEM((2 * nx, nt), bf16),
            pltpu.VMEM((2 * nx, nt), bf16),
            pltpu.VMEM((4 * nx, nt), bf16),
            pltpu.VMEM((4 * nx, nt), bf16),
            pltpu.VMEM((chunks, devices * blk, cols), f32),
            pltpu.VMEM((chunks, devices * blk, cols), f32),
            pltpu.VMEM(field.shape, f32),
            pltpu.VMEM((8, cols), f32),
            pltpu.VMEM((devices, 8, cols), f32),
            dma((rows // 2,)),
            dma((4,)),
            dma((rows // 2,)),
            dma((chunks,)),
            dma((chunks,)),
            dma((chunks,)),
            dma((chunks,)),
            dma((2,)),
        ],
        compiler_params=pltpu.CompilerParams(
            collective_id=0, has_side_effects=True, vmem_limit_bytes=60 * 1024 * 1024
        ),
    )(field, jnp.asarray(fwd), jnp.asarray(across), jnp.asarray(time), jnp.asarray(back))


def on_device(field):
    slabs = lax.axis_size("slab")
    times = lax.axis_size("tm")
    devices = slabs * times
    _, rows, ny, cols = field.shape
    nx = rows * slabs
    nt = cols * times
    if (
        ny % (devices * PIECE) == 0
        and rows % 16 == 0
        and cols == LANES
        and nt % WIDE == 0
        and times % 2 == 0
    ):
        return in_one_kernel(field, slabs, times, PIECE)

    along_x = propagator(nx, -DIFFRACT)
    along_y = propagator(ny, -DIFFRACT)
    along_t = propagator(nt, DISPERSE)
    partial_power = jnp.sum(field[0] * field[0] + field[1] * field[1])
    mean_power = lax.psum(partial_power, AXES) / (nx * ny * nt)
    scale = 1.0 / jnp.sqrt(mean_power + EPSILON)
    index_x = jnp.arange(nx, dtype=jnp.int32)
    group = ny // times
    width = group * nt // slabs
    sent = apply("qzpb,pabc->qazc", along_y, field)
    timed = lax.all_to_all(sent, "tm", split_axis=2, concat_axis=3, tiled=True)
    timed = apply("rtqT,qabT->rabt", along_t, timed)
    crossed = lax.all_to_all(
        timed.reshape(2, rows, slabs, width), "slab", split_axis=2, concat_axis=1, tiled=True
    ).reshape(2, nx, width)
    crossed = apply("qxpX,pXw->qxw", along_x, crossed)
    flat = lax.axis_index("slab") * width + jnp.arange(width, dtype=jnp.int32)
    place_y = place(lax.axis_index("tm") * group + flat // nt, ny)
    well_depth = WELL * (place(index_x, nx)[:, None] ** 2 + place_y[None, :] ** 2)
    kicked = jnp.stack(kick(crossed[0], crossed[1], scale, well_depth))
    kicked = apply("qxpX,pXw->qxw", along_x, kicked)
    timed = lax.all_to_all(
        kicked.reshape(2, nx, 1, width), "slab", split_axis=1, concat_axis=2, tiled=True
    ).reshape(2, rows, group, nt)
    timed = apply("rtqT,qabT->rabt", along_t, timed)
    home = lax.all_to_all(timed, "tm", split_axis=3, concat_axis=2, tiled=True)
    return apply("qzpb,pabc->qazc", along_y, home)


def solution(mesh):
    placed = (P(None, "slab", None, "tm"),)
    return jax.shard_map(
        on_device,
        mesh=mesh,
        in_specs=placed,
        out_specs=P(None, "slab", None, "tm"),
        check_vma=False,
    )
```

profile of v0, /device:TPU:0, one launch (start us, length us, event | category | flops | bytes accessed | tf_op | source)
XLA Modules:
  0.0 200.5 jit_solution(2294840997351783894)
XLA Ops:
  0.0 195.9 %shard_map.55 = f32[2,16,256,128]{3,2,1,0:T(8,128)} custom-call(f32[2,16,256,128]{3,2,1,0:T(8,128)} %field_ref.1, bf16[8,128,512]{2,1,0:T(8,128)(2,1)} %constant.8.clone.fwd_ref, bf16[512,256]{1,0:T(8,128)(2,1)} %constant.9.clone.across_ref, bf16[2,2,512,512]{3,2,1,0:T(8,128)(2,1)} %constant.10.clone.time_ref, bf16[8,1024,64]{2,1,0:T(8,128)(2,1)} %constant.11.clone.back_ref), custom_call_target="tpu_custom_call" | custom-call | tf_op jit(solution)/shard_map/pallas_call | solution.py:422
  195.9 4.7 %copy.7 = f32[2,16,256,128]{3,2,1,0:T(8,128)} copy(f32[2,16,256,128]{3,2,1,0:T(8,128)} %shard_map.55) | data formatting | bytes 8388608
where the time goes:
time: 201 us
  Pallas kernels  196 us (98%)
  local copies, waits for them, and re-layouts  4.65 us (2%)
    pallas_call x1, Pallas kernels, in_one_kernel(): pl.pallas_call(functools.partial(step_kernel, dims), out_shape=jax.ShapeD...  196 us
    unnamed x1, local copies, waits for them, and re-layouts  4.65 us

commit v1 on v0

v1 whole, which is shorter than its diff:
```python
import functools
import math

import ml_dtypes
import numpy as np

import jax
import jax.numpy as jnp
from jax import lax
from jax.experimental import pallas as pl
from jax.experimental.pallas import tpu as pltpu
from jax.sharding import PartitionSpec as P

TWO_PI = 2.0 * math.pi
DIFFRACT = 4.0
DISPERSE = 3.0
KERR = 0.05
WELL = 1.5
EPSILON = 1e-06
AXES = ("slab", "tm")
LANES = 128
WIDE = 256
MESH = pl.DeviceIdType.MESH


def matrix(length, strength):
    steps = np.arange(length)
    signed = np.where(2 * steps < length, steps, steps - length)
    phase = np.exp(1j * strength * (TWO_PI * signed / length) ** 2)
    response = np.fft.ifft(phase)
    return response[(steps[:, None] - steps[None, :]) % length]


def propagator(length, strength):
    whole = matrix(length, strength)
    real = jnp.asarray(whole.real.astype(np.float32))
    imag = jnp.asarray(whole.imag.astype(np.float32))
    upper = jnp.stack([real, -imag], axis=1)
    lower = jnp.stack([imag, real], axis=1)
    return jnp.stack([upper, lower])


def halves(table):
    table = table.astype(np.float32)
    high = table.astype(ml_dtypes.bfloat16)
    low = (table - high.astype(np.float32)).astype(ml_dtypes.bfloat16)
    return high, low


def blocks(whole):
    return np.block([[whole.real, -whole.imag], [whole.imag, whole.real]])


def apply(form, table, value):
    return jnp.einsum(form, table, value, precision=lax.Precision.HIGH)


def place(index, length):
    return (index.astype(jnp.float32) - (length - 1) / 2.0) / (length / 2.0)


def kick(real, imag, scale, well_depth):
    real = real * scale
    imag = imag * scale
    angle = KERR * (real * real + imag * imag) - well_depth
    turn_c = jnp.cos(angle)
    turn_s = jnp.sin(angle)
    return real * turn_c - imag * turn_s, real * turn_s + imag * turn_c


def split(value):
    high = value.astype(jnp.bfloat16)
    low = (value - high.astype(jnp.float32)).astype(jnp.bfloat16)
    return high, low


def dot(left, right):
    return jnp.dot(left, right, preferred_element_type=jnp.float32)


def left_table(table, high, low):
    n = table.shape[0] // 2
    both = dot(table, high)
    return both[:n] + both[n:] + dot(table[:n], low)


def stacked_table(table, high, low):
    return dot(table, jnp.concatenate([high, high, low], axis=0))


def home_pair(home, start, pitch, group, rows):
    sides = []
    for i in range(2):
        sides.append(
            jnp.concatenate(
                [home[pl.ds(start + q * 8 + i, group, stride=pitch), :] for q in range(2)],
                axis=0,
            )
        )
    return split(jnp.concatenate(sides, axis=1))


def step_kernel(
    dims,
    field_ref,
    fwd_ref,
    across_ref,
    time_ref,
    back_ref,
    acc,
    home_last,
    fld,
    fh,
    fl,
    fwd,
    across,
    wt,
    back,
    turn,
    send,
    recv,
    xh,
    xl,
    ysp,
    ksp,
    hsend,
    home,
    pw_send,
    pw_recv,
    load_sem,
    table_sem,
    send_sem,
    recv_sem,
    hsend_sem,
    home_sem,
    last_sem,
    pw_sem,
):
    slabs, times, rows, ny, cols, chunks = dims
    group = slabs * times
    nx, nt = slabs * rows, times * cols
    blk = 2 * rows
    pitch = turn.shape[0] // rows
    hpitch = home_last.shape[0] // group
    pairs = rows // 2
    s = lax.axis_index("slab")
    m = lax.axis_index("tm")
    me = s * times + m

    def field_copy(xp):
        part = (slice(None), pl.ds(2 * xp, 2))
        return pltpu.make_async_copy(field_ref.at[part], fld.at[part], load_sem.at[xp])

    rest_rows = pl.ds(1, chunks - 1)
    tables = [
        pltpu.make_async_copy(a, b, table_sem.at[i])
        for i, (a, b) in enumerate(
            [
                (fwd_ref.at[0], fwd.at[0]),
                (fwd_ref.at[rest_rows], fwd.at[rest_rows]),
                (across_ref, across),
                (time_ref, wt),
                (back_ref, back),
            ]
        )
    ]
    tables[0].start()
    for xp in range(pairs):
        field_copy(xp).start()

    barrier = pltpu.get_barrier_semaphore()

    def greet(k, carry):
        peer = (me + k) % group
        pl.semaphore_signal(
            barrier, inc=1, device_id=(peer // times, peer % times), device_id_type=MESH
        )
        return carry

    lax.fori_loop(1, group, greet, 0)

    half = times // 2
    side = m // half
    order = []
    for i in range(half):
        order.append([(1 - side) * half + (m + i) % half, False])
    for i in range(1, half):
        order.append([side * half + (m + i) % half, False])
    order.append([m, True])

    def to_all(make):
        for there, own in order:
            for k in range(slabs):
                if own and k == 0:
                    continue
                make((s + k) % slabs, there)

    def forward_copy(c, ds, dm, first, count):
        return pltpu.make_async_remote_copy(
            src_ref=send.at[c, pl.ds((ds * times + dm) * blk + first, count)],
            dst_ref=recv.at[c, pl.ds(me * blk + first, count)],
            send_sem=send_sem.at[c],
            recv_sem=recv_sem.at[c],
            device_id=(ds, dm),
            device_id_type=MESH,
        )

    def home_copy(c, ds, dm):
        return pltpu.make_async_remote_copy(
            src_ref=hsend.at[c, pl.ds((ds * times + dm) * blk, blk)],
            dst_ref=home.at[c, pl.ds(me * hpitch, blk)],
            send_sem=hsend_sem.at[c],
            recv_sem=home_sem.at[c],
            device_id=(ds, dm),
            device_id_type=MESH,
        )

    def last_copy(h, ds, dm):
        return pltpu.make_async_remote_copy(
            src_ref=hsend.at[chunks - 1, pl.ds((ds * times + dm) * blk + h * rows, rows)],
            dst_ref=home_last.at[pl.ds(me * hpitch + h * rows, rows)],
            send_sem=hsend_sem.at[chunks - 1],
            recv_sem=last_sem.at[h],
            device_id=(ds, dm),
            device_id_type=MESH,
        )

    def power_copy(ds, dm):
        return pltpu.make_async_remote_copy(
            src_ref=pw_send,
            dst_ref=pw_recv.at[me],
            send_sem=pw_sem.at[0],
            recv_sem=pw_sem.at[1],
            device_id=(ds, dm),
            device_id_type=MESH,
        )

    def whole(ref, first, second):
        return pltpu.make_async_remote_copy(
            src_ref=ref,
            dst_ref=ref,
            send_sem=first,
            recv_sem=second,
            device_id=(s, m),
            device_id_type=MESH,
        )

    others = pl.ds(0, (group - 1) * blk)

    def prepare(xp, total):
        field_copy(xp).wait()
        for q in range(2):
            value = jnp.concatenate([fld[q, 2 * xp], fld[q, 2 * xp + 1]], axis=1)
            high, low = split(value)
            fh[xp, pl.ds(q * ny, ny), :] = high
            fl[xp, pl.ds(q * ny, ny), :] = low
            total = total + jnp.sum((value * value).reshape(ny // 8, 8, 2 * cols), axis=0)
        return total

    def along_y(c, xp):
        result = left_table(fwd[c], fh[xp], fl[xp])
        turn[pl.ds(2 * xp * pitch, 2 * group), :] = result[:, :cols]
        turn[pl.ds((2 * xp + 1) * pitch, 2 * group), :] = result[:, cols:]

    def lay_out(c, h):
        for r in range(group):
            for q in range(2):
                send[c, pl.ds(r * blk + h * rows + q * 8, 8), :] = turn[
                    pl.ds(h * 8 * pitch + q * group + r, 8, stride=pitch), :
                ]
        for q in range(2):
            recv[c, pl.ds(me * blk + h * rows + q * 8, 8), :] = turn[
                pl.ds(h * 8 * pitch + q * group + me, 8, stride=pitch), :
            ]

    total = jnp.zeros((8, 2 * cols), jnp.float32)
    for h in range(2):
        for xp in range(h * pairs // 2, (h + 1) * pairs // 2):
            total = prepare(xp, total)
        if h == 0:
            tables[0].wait()
        else:
            for copy in tables[1:]:
                copy.start()
            tile = jnp.sum(total[:, :cols] + total[:, cols:], axis=0, keepdims=True)
            pw_send[...] = tile
            pw_recv[me] = tile
            to_all(lambda ds, dm: power_copy(ds, dm).start())
        for xp in range(h * pairs // 2, (h + 1) * pairs // 2):
            along_y(0, xp)
        lay_out(0, h)
        if h == 0:
            pl.semaphore_wait(barrier, group - 1)
        to_all(lambda ds, dm: forward_copy(0, ds, dm, h * rows, rows).start())
    tables[1].wait()

    def rest(c, carry):
        def body(xp, inner):
            along_y(c, xp)
            return inner

        lax.fori_loop(0, pairs, body, 0)
        for h in range(2):
            lay_out(c, h)
        to_all(lambda ds, dm: forward_copy(c, ds, dm, 0, blk).start())
        return carry

    lax.fori_loop(1, chunks, rest, 0)

    for copy in tables[2:]:
        copy.wait()
    other_tiles = pw_recv.at[pl.ds(0, group - 1)]
    whole(other_tiles, pw_sem.at[0], pw_sem.at[1]).wait_recv()
    power = jnp.sum(jnp.sum(pw_recv[...], axis=0), axis=(0, 1), keepdims=True)
    scale = 1.0 / jnp.sqrt(power / (nx * ny * nt) + EPSILON)
    place_x = place(lax.broadcasted_iota(jnp.int32, (nx, WIDE), 0), nx)
    square_x = place_x * place_x
    tiles = nt // WIDE
    per_tile = WIDE // cols

    def along_t(source, n):
        lanes = pl.ds(n * WIDE, WIDE)
        parts = []
        for part in range(2):
            both = dot(source[...], wt[part, 0, :, lanes])
            parts.append(
                both[: 2 * nx] + both[2 * nx :] + dot(source[: 2 * nx], wt[part, 1, :, lanes])
            )
        gr, gi = parts
        return gr[:nx] - gi[nx:], gi[:nx] + gr[nx:]

    def middle(c):
        whole(recv.at[c, others], send_sem.at[c], recv_sem.at[c]).wait_recv()
        for a in range(slabs):
            for b in range(times):
                for q in range(2):
                    row = (a * times + b) * blk + q * 8
                    got = jnp.concatenate(
                        [recv[c, pl.ds(row + h * rows, 8), :] for h in range(2)], axis=0
                    )
                    high, low = split(got)
                    xh[pl.ds(q * nx + a * rows, rows), pl.ds(b * cols, cols)] = high
                    xl[pl.ds(q * nx + a * rows, rows), pl.ds(b * cols, cols)] = low
        for n in range(tiles):
            lanes = pl.ds(n * WIDE, WIDE)
            value = left_table(across[...], xh[:, lanes], xl[:, lanes])
            high, low = split(value)
            ysp[pl.ds(0, 2 * nx), lanes] = high
            ysp[pl.ds(2 * nx, 2 * nx), lanes] = low
        y = c * group + me
        place_y = (y.astype(jnp.float32) - (ny - 1) / 2.0) / (ny / 2.0)
        well_depth = WELL * (square_x + place_y * place_y)
        for n in range(tiles):
            lanes = pl.ds(n * WIDE, WIDE)
            real, imag = along_t(ysp, n)
            real, imag = kick(real, imag, scale, well_depth)
            for q, value in enumerate((real, imag)):
                high, low = split(value)
                ksp[pl.ds(q * nx, nx), lanes] = high
                ksp[pl.ds((2 + q) * nx, nx), lanes] = low
        for n in range(tiles):
            lanes = pl.ds(n * WIDE, WIDE)
            for q, value in enumerate(along_t(ksp, n)):
                high, low = split(value)
                xh[pl.ds(q * nx, nx), lanes] = high
                xl[pl.ds(q * nx, nx), lanes] = low
        for n in range(tiles):
            lanes = pl.ds(n * WIDE, WIDE)
            value = left_table(across[...], xh[:, lanes], xl[:, lanes])
            for q in range(2):
                for a in range(slabs):
                    for b in range(per_tile):
                        dest = a * times + n * per_tile + b
                        for h in range(2):
                            first = q * nx + a * rows + h * 8
                            hsend[c, pl.ds(dest * blk + h * rows + q * 8, 8), :] = value[
                                first : first + 8, b * cols : (b + 1) * cols
                            ]

    def most(c, carry):
        middle(c)
        home[c, pl.ds(me * hpitch, blk), :] = hsend[c, pl.ds(me * blk, blk), :]
        to_all(lambda ds, dm: home_copy(c, ds, dm).start())
        return carry

    lax.fori_loop(0, chunks - 1, most, 0)
    middle(chunks - 1)
    home_last[pl.ds(me * hpitch, blk), :] = hsend[chunks - 1, pl.ds(me * blk, blk), :]
    for h in range(2):
        to_all(lambda ds, dm: last_copy(h, ds, dm).start())

    acc[...] = jnp.zeros_like(acc)

    def gather(c, carry):
        whole(home.at[c, others], hsend_sem.at[c], home_sem.at[c]).wait_recv()
        source = home.at[c]

        def add_up(xp, inner):
            start = (xp // 4) * rows + (2 * xp) % 8
            high, low = home_pair(source, start, hpitch, group, rows)
            value = stacked_table(back[c], high, low)
            for q in range(2):
                for i in range(2):
                    part = value[q * ny : (q + 1) * ny, i * cols : (i + 1) * cols]
                    acc[q, 2 * xp + i] = acc[q, 2 * xp + i] + part
            return inner

        lax.fori_loop(0, pairs, add_up, 0)
        return carry

    lax.fori_loop(0, chunks - 1, gather, 0)

    def drain(c, carry):
        whole(send.at[c, others], send_sem.at[c], recv_sem.at[c]).wait_send()
        whole(hsend.at[c, others], hsend_sem.at[c], home_sem.at[c]).wait_send()
        return carry

    lax.fori_loop(0, chunks - 1, drain, 0)
    whole(send.at[chunks - 1, others], send_sem.at[chunks - 1], recv_sem.at[chunks - 1]).wait_send()
    whole(other_tiles, pw_sem.at[0], pw_sem.at[1]).wait_send()

    half_others = pl.ds(0, (group - 1) * rows)
    whole(home_last.at[half_others], hsend_sem.at[chunks - 1], last_sem.at[0]).wait_recv()
    for xp in range(pairs // 2):
        start = (xp // 4) * rows + (2 * xp) % 8
        high, low = home_pair(home_last, start, hpitch, group, rows)
        value = stacked_table(back[chunks - 1], high, low)
        for q in range(2):
            for i in range(2):
                part = value[q * ny : (q + 1) * ny, i * cols : (i + 1) * cols]
                acc[q, 2 * xp + i] = acc[q, 2 * xp + i] + part
    whole(hsend.at[chunks - 1, others], hsend_sem.at[chunks - 1], last_sem.at[1]).wait_send()
    whole(home_last.at[half_others], hsend_sem.at[chunks - 1], last_sem.at[1]).wait_recv()


def finish_kernel(dims, acc, home_last, back, out_ref, stage, out_sem):
    group, rows, ny, cols = dims
    hpitch = home_last.shape[0] // group
    pairs = rows // 2

    def early(xp):
        part = (slice(None), pl.ds(2 * xp, 2))
        return pltpu.make_async_copy(acc.at[part], out_ref.at[part], out_sem.at[xp])

    def late(xp):
        return pltpu.make_async_copy(
            stage.at[:, pl.ds(2 * xp - rows // 2, 2)],
            out_ref.at[:, pl.ds(2 * xp, 2)],
            out_sem.at[xp],
        )

    for xp in range(pairs // 2):
        early(xp).start()
    for xp in range(pairs // 2, pairs):
        start = (xp // 4) * rows + (2 * xp) % 8
        high, low = home_pair(home_last, start, hpitch, group, rows)
        value = stacked_table(back[...], high, low)
        for q in range(2):
            for i in range(2):
                part = value[q * ny : (q + 1) * ny, i * cols : (i + 1) * cols]
                stage[q, 2 * xp - rows // 2 + i] = acc[q, 2 * xp + i] + part
        late(xp).start()
    for xp in range(pairs // 2):
        early(xp).wait()
    for xp in range(pairs // 2, pairs):
        late(xp).wait()


def in_kernels(field, slabs, times):
    _, rows, ny, cols = field.shape
    group = slabs * times
    nx, nt = rows * slabs, cols * times
    chunks = ny // group
    blk = 2 * rows
    hpitch = blk + 8
    pitch = 2 * group + 8
    uy = matrix(ny, -DIFFRACT)
    ux = matrix(nx, -DIFFRACT)
    ut = matrix(nt, DISPERSE)
    full_y = blocks(uy).reshape(2, ny, 2, ny)
    fwd, back = [], []
    for c in range(chunks):
        mine = slice(c * group, (c + 1) * group)
        fwd.append(np.concatenate(halves(full_y[:, mine].reshape(2 * group, 2 * ny))))
        high, low = halves(full_y[:, :, :, mine].reshape(2 * ny, 2 * group))
        back.append(np.concatenate([high, low, high], axis=1))
    fwd, back = np.stack(fwd), np.stack(back)
    across = np.concatenate(halves(blocks(ux)))
    time = np.stack([np.stack(halves(ut.real)), np.stack(halves(ut.imag))])
    dims = (slabs, times, rows, ny, cols, chunks)
    f32, bf16 = jnp.float32, jnp.bfloat16
    hbm = pl.BlockSpec(memory_space=pltpu.HBM)
    vmem = pl.BlockSpec(memory_space=pltpu.VMEM)
    dma = pltpu.SemaphoreType.DMA
    acc, home_last = pl.pallas_call(
        functools.partial(step_kernel, dims),
        out_shape=(
            jax.ShapeDtypeStruct(field.shape, f32),
            jax.ShapeDtypeStruct((group * hpitch, cols), f32),
        ),
        in_specs=[hbm] * 5,
        out_specs=(vmem, vmem),
        scratch_shapes=[
            pltpu.VMEM(field.shape, f32),
            pltpu.VMEM((rows // 2, 2 * ny, 2 * cols), bf16),
            pltpu.VMEM((rows // 2, 2 * ny, 2 * cols), bf16),
            pltpu.VMEM(fwd.shape, bf16),
            pltpu.VMEM(across.shape, bf16),
            pltpu.VMEM(time.shape, bf16),
            pltpu.VMEM(back.shape, bf16),
            pltpu.VMEM((rows * pitch, cols), f32),
            pltpu.VMEM((chunks, group * blk, cols), f32),
            pltpu.VMEM((chunks, group * blk, cols), f32),
            pltpu.VMEM((2 * nx, nt), bf16),
            pltpu.VMEM((2 * nx, nt), bf16),
            pltpu.VMEM((4 * nx, nt), bf16),
            pltpu.VMEM((4 * nx, nt), bf16),
            pltpu.VMEM((chunks, group * blk, cols), f32),
            pltpu.VMEM((chunks - 1, group * hpitch, cols), f32),
            pltpu.VMEM((1, cols), f32),
            pltpu.VMEM((group, 1, cols), f32),
            dma((rows // 2,)),
            dma((5,)),
            dma((chunks,)),
            dma((chunks,)),
            dma((chunks,)),
            dma((chunks - 1,)),
            dma((2,)),
            dma((2,)),
        ],
        compiler_params=pltpu.CompilerParams(
            collective_id=0, has_side_effects=True, vmem_limit_bytes=48 * 1024 * 1024
        ),
    )(field, *[pltpu.with_memory_space_constraint(jnp.asarray(a), pltpu.HBM) for a in (fwd, across, time, back)])
    return pl.pallas_call(
        functools.partial(finish_kernel, (group, rows, ny, cols)),
        out_shape=jax.ShapeDtypeStruct(field.shape, f32),
        in_specs=[vmem] * 3,
        out_specs=hbm,
        scratch_shapes=[
            pltpu.VMEM((2, rows // 2, ny, cols), f32),
            dma((rows // 2,)),
        ],
        compiler_params=pltpu.CompilerParams(vmem_limit_bytes=16 * 1024 * 1024),
    )(acc, home_last, jnp.asarray(back[-1]))


def on_device(field):
    slabs = lax.axis_size("slab")
    times = lax.axis_size("tm")
    devices = slabs * times
    _, rows, ny, cols = field.shape
    nx = rows * slabs
    nt = cols * times
    if (
        ny % devices == 0
        and ny // devices > 2
        and devices % 8 == 0
        and rows == 16
        and cols == LANES
        and nt % WIDE == 0
        and times % 2 == 0
    ):
        return in_kernels(field, slabs, times)

    along_x = propagator(nx, -DIFFRACT)
    along_y = propagator(ny, -DIFFRACT)
    along_t = propagator(nt, DISPERSE)
    partial_power = jnp.sum(field[0] * field[0] + field[1] * field[1])
    mean_power = lax.psum(partial_power, AXES) / (nx * ny * nt)
    scale = 1.0 / jnp.sqrt(mean_power + EPSILON)
    index_x = jnp.arange(nx, dtype=jnp.int32)
    group = ny // times
    width = group * nt // slabs
    sent = apply("qzpb,pabc->qazc", along_y, field)
    timed = lax.all_to_all(sent, "tm", split_axis=2, concat_axis=3, tiled=True)
    timed = apply("rtqT,qabT->rabt", along_t, timed)
    crossed = lax.all_to_all(
        timed.reshape(2, rows, slabs, width), "slab", split_axis=2, concat_axis=1, tiled=True
    ).reshape(2, nx, width)
    crossed = apply("qxpX,pXw->qxw", along_x, crossed)
    flat = lax.axis_index("slab") * width + jnp.arange(width, dtype=jnp.int32)
    place_y = place(lax.axis_index("tm") * group + flat // nt, ny)
    well_depth = WELL * (place(index_x, nx)[:, None] ** 2 + place_y[None, :] ** 2)
    kicked = jnp.stack(kick(crossed[0], crossed[1], scale, well_depth))
    kicked = apply("qxpX,pXw->qxw", along_x, kicked)
    timed = lax.all_to_all(
        kicked.reshape(2, nx, 1, width), "slab", split_axis=1, concat_axis=2, tiled=True
    ).reshape(2, rows, group, nt)
    timed = apply("rtqT,qabT->rabt", along_t, timed)
    home = lax.all_to_all(timed, "tm", split_axis=3, concat_axis=2, tiled=True)
    return apply("qzpb,pabc->qazc", along_y, home)


def solution(mesh):
    placed = (P(None, "slab", None, "tm"),)
    return jax.shard_map(
        on_device,
        mesh=mesh,
        in_specs=placed,
        out_specs=P(None, "slab", None, "tm"),
        check_vma=False,
    )
```

time: 201 us -> 191 us (0.950)
  Pallas kernels: 196 us -> 191 us
  local copies, waits for them, and re-layouts: 4.65 us -> 0.01 us
    pallas_call x1 -> x2, Pallas kernels: 196 us -> 191 us  [the longest x1 189 us: in_kernels(): pl.pallas_call(functools.partial(step_kernel, dims), out_shape=(jax.Shape...]
    unnamed x1 -> x2, local copies, waits for them, and re-layouts: 4.65 us -> 0.01 us
where the time goes in v1:
time: 191 us
  Pallas kernels  191 us (100%)
    pallas_call x1, Pallas kernels, in_kernels(): pl.pallas_call(functools.partial(step_kernel, dims), out_shape=(jax.Shape...  189 us

profile of v1, /device:TPU:0, one launch (start us, length us, event | category | flops | bytes accessed | tf_op | source)
XLA Modules:
  0.0 190.7 jit_solution(9106967395148878182)
XLA Ops:
  0.0 0.0 copy-start
  0.0 188.6 %shard_map.64 = (f32[2,16,256,128]{3,2,1,0:T(8,128)S(1)}, f32[1280,128]{1,0:T(8,128)S(1)}) custom-call(f32[2,16,256,128]{3,2,1,0:T(8,128)} %field_ref.1, bf16[8,128,512]{2,1,0:T(8,128)(2,1)} %constant.10.clone.fwd_ref, bf16[512,256]{1,0:T(8,128)(2,1)} %constant.11.clone.across_ref, bf16[2,2,512,512]{3,2,1,0:T(8,128)(2,1)} %constant.12.clone.time_ref, ...), custom_call_target="tpu_custom_call" | custom-call | tf_op jit(solution)/shard_map/pallas_call | solution.py:495
  188.6 0.0 copy-done
  188.6 2.1 %shard_map.65 = f32[2,16,256,128]{3,2,1,0:T(8,128)} custom-call(f32[2,16,256,128]{3,2,1,0:T(8,128)S(1)} %get-tuple-element.7.acc, f32[1280,128]{1,0:T(8,128)S(1)} %get-tuple-element.8.home_last, bf16[512,192]{1,0:T(8,128)(2,1)S(1)} %copy-done), custom_call_target="tpu_custom_call" | custom-call | tf_op jit(solution)/shard_map/pallas_call | solution.py:535
Async XLA Ops:
  0.0 188.6 %copy-start = (bf16[512,192]{1,0:T(8,128)(2,1)S(1)}, bf16[512,192]{1,0:T(8,128)(2,1)}, u32[]{:S(2)}) copy-start(bf16[512,192]{1,0:T(8,128)(2,1)} %constant.14.clone.back) | copy-start | bytes 589828

commit v2 on v1

v2 whole, which is shorter than its diff:
```python
import functools
import math

import ml_dtypes
import numpy as np

import jax
import jax.numpy as jnp
from jax import lax
from jax.experimental import pallas as pl
from jax.experimental.pallas import tpu as pltpu
from jax.sharding import PartitionSpec as P

TWO_PI = 2.0 * math.pi
DIFFRACT = 4.0
DISPERSE = 3.0
KERR = 0.05
WELL = 1.5
EPSILON = 1e-06
AXES = ("slab", "tm")
LANES = 128
WIDE = 256
MESH = pl.DeviceIdType.MESH


def matrix(length, strength):
    steps = np.arange(length)
    signed = np.where(2 * steps < length, steps, steps - length)
    phase = np.exp(1j * strength * (TWO_PI * signed / length) ** 2)
    response = np.fft.ifft(phase)
    return response[(steps[:, None] - steps[None, :]) % length]


def propagator(length, strength):
    whole = matrix(length, strength)
    real = jnp.asarray(whole.real.astype(np.float32))
    imag = jnp.asarray(whole.imag.astype(np.float32))
    upper = jnp.stack([real, -imag], axis=1)
    lower = jnp.stack([imag, real], axis=1)
    return jnp.stack([upper, lower])


def halves(table):
    table = table.astype(np.float32)
    high = table.astype(ml_dtypes.bfloat16)
    low = (table - high.astype(np.float32)).astype(ml_dtypes.bfloat16)
    return high, low


def blocks(whole):
    return np.block([[whole.real, -whole.imag], [whole.imag, whole.real]])


def apply(form, table, value):
    return jnp.einsum(form, table, value, precision=lax.Precision.HIGH)


def place(index, length):
    return (index.astype(jnp.float32) - (length - 1) / 2.0) / (length / 2.0)


def kick(real, imag, scale, well_depth):
    real = real * scale
    imag = imag * scale
    angle = KERR * (real * real + imag * imag) - well_depth
    turn_c = jnp.cos(angle)
    turn_s = jnp.sin(angle)
    return real * turn_c - imag * turn_s, real * turn_s + imag * turn_c


def split(value):
    high = value.astype(jnp.bfloat16)
    low = (value - high.astype(jnp.float32)).astype(jnp.bfloat16)
    return high, low


def dot(left, right):
    return jnp.dot(left, right, preferred_element_type=jnp.float32)


def left_table(table, high, low):
    n = table.shape[0] // 2
    both = dot(table, high)
    return both[:n] + both[n:] + dot(table[:n], low)


def stacked_table(table, high, low):
    return dot(table, jnp.concatenate([high, high, low], axis=0))


def home_pair(home, h, first, slabs, times):
    sides = []
    for i in range(2):
        pieces = []
        for q in range(2):
            for b in range(times):
                start = ((b * 2 + h) * slabs * 2 + q) * 8 + first + i
                pieces.append(home[pl.ds(start, slabs, stride=16), :])
        sides.append(jnp.concatenate(pieces, axis=0))
    return split(jnp.concatenate(sides, axis=1))


def step_kernel(
    dims,
    field_ref,
    fwd_ref,
    across_ref,
    time_ref,
    back_ref,
    acc,
    home,
    fld,
    fh,
    fl,
    fwd,
    across,
    wt,
    back,
    turn,
    zsend,
    zrecv,
    asend,
    arecv,
    bsend,
    brecv,
    hsend,
    ysp,
    pw_send,
    pw_recv,
    pw_all,
    load_sem,
    table_sem,
    zsend_sem,
    zrecv_sem,
    asend_sem,
    arecv_sem,
    bsend_sem,
    brecv_sem,
    hsend_sem,
    home_sem,
    pw_sem,
):
    slabs, times, rows, ny, cols, chunks = dims
    group = slabs * times
    nx, nt = slabs * rows, times * cols
    blk = 2 * rows
    zhalf = slabs * rows
    zblk = 2 * zhalf
    pitch = turn.shape[0] // rows
    pairs = rows // 2
    some = pairs // 2
    s = lax.axis_index("slab")
    m = lax.axis_index("tm")

    def field_copy(xp):
        part = (slice(None), pl.ds(2 * xp, 2))
        return pltpu.make_async_copy(field_ref.at[part], fld.at[part], load_sem.at[xp])

    rest_rows = pl.ds(1, chunks - 1)
    tables = [
        pltpu.make_async_copy(a, b, table_sem.at[i])
        for i, (a, b) in enumerate(
            [
                (fwd_ref.at[0], fwd.at[0]),
                (fwd_ref.at[rest_rows], fwd.at[rest_rows]),
                (across_ref, across),
                (time_ref, wt),
                (back_ref, back),
            ]
        )
    ]
    tables[0].start()
    for xp in range(pairs):
        field_copy(xp).start()

    half = times // 2
    side = m // half
    line = [(1 - side) * half + (m + i) % half for i in range(half)]
    line = line + [side * half + (m + i) % half for i in range(1, half)]
    ring = [(s + k) % slabs for k in range(1, slabs)]

    barrier = pltpu.get_barrier_semaphore()
    for there in line:
        pl.semaphore_signal(barrier, inc=1, device_id=(s, there), device_id_type=MESH)
    for there in ring:
        pl.semaphore_signal(barrier, inc=1, device_id=(there, m), device_id_type=MESH)

    def remote(src, dst, first, second, device):
        return pltpu.make_async_remote_copy(
            src_ref=src,
            dst_ref=dst,
            send_sem=first,
            recv_sem=second,
            device_id=device,
            device_id_type=MESH,
        )

    def whole(ref, first, second):
        return remote(ref, ref, first, second, (s, m))

    def out_along_t(c, h):
        for there in line:
            remote(
                zsend.at[c, pl.ds(there * zblk + h * zhalf, zhalf)],
                zrecv.at[c, pl.ds(m * zblk + h * zhalf, zhalf)],
                zsend_sem.at[c],
                zrecv_sem.at[c],
                (s, there),
            ).start()

    def out_across(c):
        for there in ring:
            remote(
                asend.at[c, pl.ds(there * blk, blk)],
                arecv.at[c, pl.ds(s * blk, blk)],
                asend_sem.at[c],
                arecv_sem.at[c],
                (there, m),
            ).start()

    def home_across(c):
        for there in ring:
            remote(
                bsend.at[c, pl.ds(there * blk, blk)],
                brecv.at[c, pl.ds(s * blk, blk)],
                bsend_sem.at[c],
                brecv_sem.at[c],
                (there, m),
            ).start()

    def home_along_t(c, h):
        for there in line:
            remote(
                hsend.at[c, pl.ds(there * zblk + h * zhalf, zhalf)],
                home.at[c, pl.ds(m * zblk + h * zhalf, zhalf)],
                hsend_sem.at[c],
                home_sem.at[c, h],
                (s, there),
            ).start()

    z_others = pl.ds(0, (times - 1) * zblk)
    z_half_others = pl.ds(0, (times - 1) * zhalf)
    a_others = pl.ds(0, (slabs - 1) * blk)

    def prepare(xp, total):
        field_copy(xp).wait()
        for q in range(2):
            value = jnp.concatenate([fld[q, 2 * xp], fld[q, 2 * xp + 1]], axis=1)
            high, low = split(value)
            fh[xp, pl.ds(q * ny, ny), :] = high
            fl[xp, pl.ds(q * ny, ny), :] = low
            total = total + jnp.sum((value * value).reshape(ny // 8, 8, 2 * cols), axis=0)
        return total

    def along_y(c, xp):
        result = left_table(fwd[c], fh[xp], fl[xp])
        turn[pl.ds(2 * xp * pitch, 2 * group), :] = result[:, :cols]
        turn[pl.ds((2 * xp + 1) * pitch, 2 * group), :] = result[:, cols:]

    def lay_out(c, h):
        for there in range(times):
            for k in range(slabs):
                for q in range(2):
                    zsend[c, pl.ds(there * zblk + h * zhalf + k * rows + q * 8, 8), :] = turn[
                        pl.ds(h * 8 * pitch + q * group + there * slabs + k, 8, stride=pitch), :
                    ]
        mine = pl.ds(m * zblk + h * zhalf, zhalf)
        zrecv[c, mine, :] = zsend[c, mine, :]

    total = jnp.zeros((8, 2 * cols), jnp.float32)
    for h in range(2):
        for xp in range(h * some, (h + 1) * some):
            total = prepare(xp, total)
        if h == 0:
            tables[0].wait()
        else:
            for copy in tables[1:]:
                copy.start()
            tile = jnp.sum(total[:, :cols] + total[:, cols:], axis=0, keepdims=True)
            pw_send[0] = tile
            pw_recv[s] = tile
            for there in ring:
                remote(
                    pw_send.at[0], pw_recv.at[s], pw_sem.at[0], pw_sem.at[1], (there, m)
                ).start()
        for xp in range(h * some, (h + 1) * some):
            along_y(0, xp)
        lay_out(0, h)
        if h == 0:
            pl.semaphore_wait(barrier, times - 1 + slabs - 1)
        out_along_t(0, h)
    slab_tiles = pw_recv.at[pl.ds(0, slabs - 1)]
    whole(slab_tiles, pw_sem.at[0], pw_sem.at[1]).wait_recv()
    tile = jnp.sum(pw_recv[...], axis=0)
    pw_send[1] = tile
    pw_all[m] = tile
    for there in line:
        remote(pw_send.at[1], pw_all.at[m], pw_sem.at[2], pw_sem.at[3], (s, there)).start()
    tables[1].wait()

    def rest(c, carry):
        def body(xp, inner):
            along_y(c, xp)
            return inner

        lax.fori_loop(0, pairs, body, 0)
        for h in range(2):
            lay_out(c, h)
            out_along_t(c, h)
        return carry

    lax.fori_loop(1, chunks, rest, 0)

    for copy in tables[2:]:
        copy.wait()
    line_tiles = pw_all.at[pl.ds(0, times - 1)]
    whole(line_tiles, pw_sem.at[2], pw_sem.at[3]).wait_recv()
    power = jnp.sum(jnp.sum(pw_all[...], axis=0), axis=(0, 1), keepdims=True)
    scale = 1.0 / jnp.sqrt(power / (nx * ny * nt) + EPSILON)
    sets = 2 * slabs
    position = lax.broadcasted_iota(jnp.int32, (sets, 8, WIDE), 0) * 8
    position = position + lax.broadcasted_iota(jnp.int32, (sets, 8, WIDE), 1)
    place_x = place(position, nx)
    square_x = place_x * place_x
    tiles = nt // WIDE
    per_tile = WIDE // cols

    def parts_of(value):
        value = value.reshape(sets, 2, 8, WIDE)
        return value[:, 0], value[:, 1]

    def along_t(n):
        lanes = pl.ds(n * WIDE, WIDE)
        products = []
        for part in range(2):
            both = dot(ysp[...], wt[part, 0, :, lanes])
            low = dot(ysp[: 2 * nx], wt[part, 1, :, lanes])
            products.append(parts_of(both[: 2 * nx] + both[2 * nx :] + low))
        (rr, ir), (ri, ii) = products
        return rr - ii, ri + ir

    def first_t(c):
        whole(zrecv.at[c, z_others], zsend_sem.at[c], zrecv_sem.at[c]).wait_recv()
        for b in range(times):
            high, low = split(zrecv[c, pl.ds(b * zblk, zblk), :])
            ysp[pl.ds(0, 2 * nx), pl.ds(b * cols, cols)] = high
            ysp[pl.ds(2 * nx, 2 * nx), pl.ds(b * cols, cols)] = low
        for n in range(tiles):
            lanes = pl.ds(n * WIDE, WIDE)
            for q, value in enumerate(along_t(n)):
                for h in range(2):
                    for k in range(slabs):
                        asend[c, pl.ds(k * blk + h * rows + q * 8, 8), lanes] = value[h * slabs + k]
        mine = pl.ds(s * blk, blk)
        arecv[c, mine, :] = asend[c, mine, :]
        out_across(c)

    def centre(c):
        whole(arecv.at[c, a_others], asend_sem.at[c], arecv_sem.at[c]).wait_recv()
        y = c * group + m * slabs + s
        place_y = (y.astype(jnp.float32) - (ny - 1) / 2.0) / (ny / 2.0)
        well_depth = WELL * (square_x + place_y * place_y)
        for n in range(tiles):
            lanes = pl.ds(n * WIDE, WIDE)
            real, imag = parts_of(left_table(across[...], *split(arecv[c, :, lanes])))
            real, imag = kick(real, imag, scale, well_depth)
            value = jnp.stack([real, imag], axis=1).reshape(2 * nx, WIDE)
            bsend[c, :, lanes] = left_table(across[...], *split(value))
        mine = pl.ds(s * blk, blk)
        brecv[c, mine, :] = bsend[c, mine, :]
        home_across(c)

    def second_t(c):
        whole(brecv.at[c, a_others], bsend_sem.at[c], brecv_sem.at[c]).wait_recv()
        high, low = split(brecv[c])
        ysp[pl.ds(0, 2 * nx), :] = high
        ysp[pl.ds(2 * nx, 2 * nx), :] = low
        for n in range(tiles):
            for q, value in enumerate(along_t(n)):
                for h in range(2):
                    for k in range(slabs):
                        for b in range(per_tile):
                            row = (n * per_tile + b) * zblk + h * zhalf + k * rows + q * 8
                            hsend[c, pl.ds(row, 8), :] = value[
                                k * 2 + h, :, b * cols : (b + 1) * cols
                            ]
        mine = pl.ds(m * zblk, zblk)
        home[c, mine, :] = hsend[c, mine, :]
        for h in range(2):
            home_along_t(c, h)

    def pipeline(i, carry):
        @pl.when(i < chunks)
        def _():
            first_t(i)

        @pl.when(jnp.logical_and(i >= 1, i < chunks + 1))
        def _():
            centre(i - 1)

        @pl.when(i >= 2)
        def _():
            second_t(i - 2)

        return carry

    lax.fori_loop(0, chunks + 2, pipeline, 0)

    acc[...] = jnp.zeros_like(acc)

    def add_up(c, source, h, xp, first):
        high, low = home_pair(source, h, first, slabs, times)
        value = stacked_table(back[c], high, low)
        for q in range(2):
            for i in range(2):
                part = value[q * ny : (q + 1) * ny, i * cols : (i + 1) * cols]
                acc[q, 2 * xp + i] = acc[q, 2 * xp + i] + part

    def gather(c, carry):
        source = home.at[c]
        for h in range(2):
            whole(home.at[c, z_half_others], hsend_sem.at[c], home_sem.at[c, h]).wait_recv()

            def body(k, inner):
                add_up(c, source, h, h * some + k, 2 * k)
                return inner

            lax.fori_loop(0, some, body, 0)
        return carry

    lax.fori_loop(0, chunks - 1, gather, 0)

    last = chunks - 1

    def drain(c, carry):
        whole(zsend.at[c, z_others], zsend_sem.at[c], zrecv_sem.at[c]).wait_send()
        whole(asend.at[c, a_others], asend_sem.at[c], arecv_sem.at[c]).wait_send()
        whole(bsend.at[c, a_others], bsend_sem.at[c], brecv_sem.at[c]).wait_send()
        return carry

    lax.fori_loop(0, chunks, drain, 0)
    whole(slab_tiles, pw_sem.at[0], pw_sem.at[1]).wait_send()
    whole(line_tiles, pw_sem.at[2], pw_sem.at[3]).wait_send()

    def drain_home(c, carry):
        whole(hsend.at[c, z_others], hsend_sem.at[c], home_sem.at[c, 0]).wait_send()
        return carry

    lax.fori_loop(0, last, drain_home, 0)
    whole(home.at[last, z_half_others], hsend_sem.at[last], home_sem.at[last, 0]).wait_recv()
    for xp in range(some):
        add_up(last, home.at[last], 0, xp, 2 * xp)
    drain_home(last, 0)
    whole(home.at[last, z_half_others], hsend_sem.at[last], home_sem.at[last, 1]).wait_recv()


def finish_kernel(dims, acc, home, back, out_ref, stage, out_sem):
    slabs, times, rows, ny, cols, chunks = dims
    pairs = rows // 2
    some = pairs // 2

    def early(xp):
        part = (slice(None), pl.ds(2 * xp, 2))
        return pltpu.make_async_copy(acc.at[part], out_ref.at[part], out_sem.at[xp])

    def late(k):
        return pltpu.make_async_copy(
            stage.at[:, pl.ds(2 * k, 2)],
            out_ref.at[:, pl.ds(rows // 2 + 2 * k, 2)],
            out_sem.at[some + k],
        )

    for xp in range(some):
        early(xp).start()
    for k in range(some):
        high, low = home_pair(home.at[chunks - 1], 1, 2 * k, slabs, times)
        value = stacked_table(back[...], high, low)
        for q in range(2):
            for i in range(2):
                part = value[q * ny : (q + 1) * ny, i * cols : (i + 1) * cols]
                stage[q, 2 * k + i] = acc[q, rows // 2 + 2 * k + i] + part
        late(k).start()
    for xp in range(some):
        early(xp).wait()
    for k in range(some):
        late(k).wait()


def in_kernels(field, slabs, times):
    _, rows, ny, cols = field.shape
    group = slabs * times
    nx, nt = rows * slabs, cols * times
    chunks = ny // group
    blk = 2 * rows
    pitch = 2 * group + 8
    uy = matrix(ny, -DIFFRACT)
    ux = matrix(nx, -DIFFRACT)
    ut = matrix(nt, DISPERSE)
    full_y = blocks(uy).reshape(2, ny, 2, ny)
    fwd, back = [], []
    for c in range(chunks):
        mine = slice(c * group, (c + 1) * group)
        fwd.append(np.concatenate(halves(full_y[:, mine].reshape(2 * group, 2 * ny))))
        high, low = halves(full_y[:, :, :, mine].reshape(2 * ny, 2 * group))
        back.append(np.concatenate([high, low, high], axis=1))
    fwd, back = np.stack(fwd), np.stack(back)
    full_x = blocks(ux).reshape(2, 2 * slabs, 8, 2, 2 * slabs, 8).transpose(1, 0, 2, 4, 3, 5)
    across = np.concatenate(halves(full_x.reshape(2 * nx, 2 * nx)))
    time = np.stack([np.stack(halves(ut.real)), np.stack(halves(ut.imag))])
    dims = (slabs, times, rows, ny, cols, chunks)
    f32, bf16 = jnp.float32, jnp.bfloat16
    hbm = pl.BlockSpec(memory_space=pltpu.HBM)
    vmem = pl.BlockSpec(memory_space=pltpu.VMEM)
    dma = pltpu.SemaphoreType.DMA
    narrow = (chunks, group * blk, cols)
    wide = (chunks, slabs * blk, nt)
    tables = [jnp.asarray(a) for a in (fwd, across, time, back)]
    acc, home = pl.pallas_call(
        functools.partial(step_kernel, dims),
        out_shape=(
            jax.ShapeDtypeStruct(field.shape, f32),
            jax.ShapeDtypeStruct(narrow, f32),
        ),
        in_specs=[hbm] * 5,
        out_specs=(vmem, vmem),
        scratch_shapes=[
            pltpu.VMEM(field.shape, f32),
            pltpu.VMEM((rows // 2, 2 * ny, 2 * cols), bf16),
            pltpu.VMEM((rows // 2, 2 * ny, 2 * cols), bf16),
            pltpu.VMEM(fwd.shape, bf16),
            pltpu.VMEM(across.shape, bf16),
            pltpu.VMEM(time.shape, bf16),
            pltpu.VMEM(back.shape, bf16),
            pltpu.VMEM((rows * pitch, cols), f32),
            pltpu.VMEM(narrow, f32),
            pltpu.VMEM(narrow, f32),
            pltpu.VMEM(wide, f32),
            pltpu.VMEM(wide, f32),
            pltpu.VMEM(wide, f32),
            pltpu.VMEM(wide, f32),
            pltpu.VMEM(narrow, f32),
            pltpu.VMEM((4 * nx, nt), bf16),
            pltpu.VMEM((2, 1, cols), f32),
            pltpu.VMEM((slabs, 1, cols), f32),
            pltpu.VMEM((times, 1, cols), f32),
            dma((rows // 2,)),
            dma((5,)),
            dma((chunks,)),
            dma((chunks,)),
            dma((chunks,)),
            dma((chunks,)),
            dma((chunks,)),
            dma((chunks,)),
            dma((chunks,)),
            dma((chunks, 2)),
            dma((4,)),
        ],
        compiler_params=pltpu.CompilerParams(
            collective_id=0, has_side_effects=True, vmem_limit_bytes=45 * 1024 * 1024
        ),
    )(field, *[pltpu.with_memory_space_constraint(a, pltpu.HBM) for a in tables])
    return pl.pallas_call(
        functools.partial(finish_kernel, dims),
        out_shape=jax.ShapeDtypeStruct(field.shape, f32),
        in_specs=[vmem] * 3,
        out_specs=hbm,
        scratch_shapes=[
            pltpu.VMEM((2, rows // 2, ny, cols), f32),
            dma((rows // 2,)),
        ],
        compiler_params=pltpu.CompilerParams(vmem_limit_bytes=16 * 1024 * 1024),
    )(acc, home, jnp.asarray(back[-1]))


def on_device(field):
    slabs = lax.axis_size("slab")
    times = lax.axis_size("tm")
    devices = slabs * times
    _, rows, ny, cols = field.shape
    nx = rows * slabs
    nt = cols * times
    if (
        ny % devices == 0
        and ny // devices > 2
        and slabs == 8
        and rows == 16
        and cols == LANES
        and nt % WIDE == 0
        and times % 2 == 0
    ):
        return in_kernels(field, slabs, times)

    along_x = propagator(nx, -DIFFRACT)
    along_y = propagator(ny, -DIFFRACT)
    along_t = propagator(nt, DISPERSE)
    partial_power = jnp.sum(field[0] * field[0] + field[1] * field[1])
    mean_power = lax.psum(partial_power, AXES) / (nx * ny * nt)
    scale = 1.0 / jnp.sqrt(mean_power + EPSILON)
    index_x = jnp.arange(nx, dtype=jnp.int32)
    group = ny // times
    width = group * nt // slabs
    sent = apply("qzpb,pabc->qazc", along_y, field)
    timed = lax.all_to_all(sent, "tm", split_axis=2, concat_axis=3, tiled=True)
    timed = apply("rtqT,qabT->rabt", along_t, timed)
    crossed = lax.all_to_all(
        timed.reshape(2, rows, slabs, width), "slab", split_axis=2, concat_axis=1, tiled=True
    ).reshape(2, nx, width)
    crossed = apply("qxpX,pXw->qxw", along_x, crossed)
    flat = lax.axis_index("slab") * width + jnp.arange(width, dtype=jnp.int32)
    place_y = place(lax.axis_index("tm") * group + flat // nt, ny)
    well_depth = WELL * (place(index_x, nx)[:, None] ** 2 + place_y[None, :] ** 2)
    kicked = jnp.stack(kick(crossed[0], crossed[1], scale, well_depth))
    kicked = apply("qxpX,pXw->qxw", along_x, kicked)
    timed = lax.all_to_all(
        kicked.reshape(2, nx, 1, width), "slab", split_axis=1, concat_axis=2, tiled=True
    ).reshape(2, rows, group, nt)
    timed = apply("rtqT,qabT->rabt", along_t, timed)
    home = lax.all_to_all(timed, "tm", split_axis=3, concat_axis=2, tiled=True)
    return apply("qzpb,pabc->qazc", along_y, home)


def solution(mesh):
    placed = (P(None, "slab", None, "tm"),)
    return jax.shard_map(
        on_device,
        mesh=mesh,
        in_specs=placed,
        out_specs=P(None, "slab", None, "tm"),
        check_vma=False,
    )
```

time: 191 us -> 190 us (level)
  no operation moved by 1% of the time
where the time goes in v2:
time: 190 us
  Pallas kernels  190 us (100%)
    pallas_call x1, Pallas kernels, in_kernels(): pl.pallas_call(functools.partial(step_kernel, dims), out_shape=(jax.Shape...  187 us

profile of v2, /device:TPU:0, one launch (start us, length us, event | category | flops | bytes accessed | tf_op | source)
XLA Modules:
  0.0 189.6 jit_solution(4984785745187143842)
XLA Ops:
  0.0 0.0 copy-start
  0.0 187.4 %shard_map.64 = (f32[2,16,256,128]{3,2,1,0:T(8,128)S(1)}, f32[8,1024,128]{2,1,0:T(8,128)S(1)}) custom-call(f32[2,16,256,128]{3,2,1,0:T(8,128)} %field_ref.1, bf16[8,128,512]{2,1,0:T(8,128)(2,1)} %constant.10.clone.fwd_ref, bf16[512,256]{1,0:T(8,128)(2,1)} %constant.11.clone.across_ref, bf16[2,2,512,512]{3,2,1,0:T(8,128)(2,1)} %constant.12.clone.time_ref, ...), custom_call_target="tpu_custom_call" | custom-call | tf_op jit(solution)/shard_map/pallas_call | solution.py:518
  187.5 0.0 copy-done
  187.5 2.1 %shard_map.65 = f32[2,16,256,128]{3,2,1,0:T(8,128)} custom-call(f32[2,16,256,128]{3,2,1,0:T(8,128)S(1)} %get-tuple-element.7.acc, f32[8,1024,128]{2,1,0:T(8,128)S(1)} %get-tuple-element.8.home, bf16[512,192]{1,0:T(8,128)(2,1)S(1)} %copy-done), custom_call_target="tpu_custom_call" | custom-call | tf_op jit(solution)/shard_map/pallas_call | solution.py:562
Async XLA Ops:
  0.0 187.5 %copy-start = (bf16[512,192]{1,0:T(8,128)(2,1)S(1)}, bf16[512,192]{1,0:T(8,128)(2,1)}, u32[]{:S(2)}) copy-start(bf16[512,192]{1,0:T(8,128)(2,1)} %constant.14.clone.back) | copy-start | bytes 589828

commit v3 on v2

--- a/solution.py
+++ b/solution.py
@@ -170,13 +170,15 @@
         )
     ]
     tables[0].start()
-    for xp in range(pairs):
+    for xp in range(some):
         field_copy(xp).start()
 
     half = times // 2
     side = m // half
-    line = [(1 - side) * half + (m + i) % half for i in range(half)]
-    line = line + [side * half + (m + i) % half for i in range(1, half)]
+    cross = [(1 - side) * half + i for i in range(half)]
+    near = [side * half + (m + i) % half for i in range(1, half)]
+    line = cross + near
+    line_home = cross[:1] + near + cross[1:]
     ring = [(s + k) % slabs for k in range(1, slabs)]
 
     barrier = pltpu.get_barrier_semaphore()
@@ -198,11 +200,11 @@
     def whole(ref, first, second):
         return remote(ref, ref, first, second, (s, m))
 
-    def out_along_t(c, h):
+    def out_along_t(c, first, count):
         for there in line:
             remote(
-                zsend.at[c, pl.ds(there * zblk + h * zhalf, zhalf)],
-                zrecv.at[c, pl.ds(m * zblk + h * zhalf, zhalf)],
+                zsend.at[c, pl.ds(there * zblk + first, count)],
+                zrecv.at[c, pl.ds(m * zblk + first, count)],
                 zsend_sem.at[c],
                 zrecv_sem.at[c],
                 (s, there),
@@ -228,15 +230,14 @@
                 (there, m),
             ).start()
 
-    def home_along_t(c, h):
-        for there in line:
-            remote(
-                hsend.at[c, pl.ds(there * zblk + h * zhalf, zhalf)],
-                home.at[c, pl.ds(m * zblk + h * zhalf, zhalf)],
-                hsend_sem.at[c],
-                home_sem.at[c, h],
-                (s, there),
-            ).start()
+    def home_along_t(c, there, first, count, arrived):
+        remote(
+            hsend.at[c, pl.ds(there * zblk + first, count)],
+            home.at[c, pl.ds(m * zblk + first, count)],
+            hsend_sem.at[c],
+            arrived,
+            (s, there),
+        ).start()
 
     z_others = pl.ds(0, (times - 1) * zblk)
     z_half_others = pl.ds(0, (times - 1) * zhalf)
@@ -271,6 +272,8 @@
     for h in range(2):
         for xp in range(h * some, (h + 1) * some):
             total = prepare(xp, total)
+            if xp < some:
+                field_copy(some + xp).start()
         if h == 0:
             tables[0].wait()
         else:
@@ -288,7 +291,7 @@
         lay_out(0, h)
         if h == 0:
             pl.semaphore_wait(barrier, times - 1 + slabs - 1)
-        out_along_t(0, h)
+        out_along_t(0, h * zhalf, zhalf)
     slab_tiles = pw_recv.at[pl.ds(0, slabs - 1)]
     whole(slab_tiles, pw_sem.at[0], pw_sem.at[1]).wait_recv()
     tile = jnp.sum(pw_recv[...], axis=0)
@@ -306,7 +309,7 @@
         lax.fori_loop(0, pairs, body, 0)
         for h in range(2):
             lay_out(c, h)
-            out_along_t(c, h)
+        out_along_t(c, 0, zblk)
         return carry
 
     lax.fori_loop(1, chunks, rest, 0)
@@ -386,8 +389,17 @@
                             ]
         mine = pl.ds(m * zblk, zblk)
         home[c, mine, :] = hsend[c, mine, :]
-        for h in range(2):
-            home_along_t(c, h)
+
+        @pl.when(c < chunks - 1)
+        def _():
+            for there in line_home:
+                home_along_t(c, there, 0, zblk, home_sem.at[c])
+
+        @pl.when(c == chunks - 1)
+        def _():
+            for there in line_home:
+                for h in range(2):
+                    home_along_t(c, there, h * zhalf, zhalf, home_sem.at[c + h])
 
     def pipeline(i, carry):
         @pl.when(i < chunks)
@@ -418,8 +430,8 @@
 
     def gather(c, carry):
         source = home.at[c]
+        whole(home.at[c, z_others], hsend_sem.at[c], home_sem.at[c]).wait_recv()
         for h in range(2):
-            whole(home.at[c, z_half_others], hsend_sem.at[c], home_sem.at[c, h]).wait_recv()
 
             def body(k, inner):
                 add_up(c, source, h, h * some + k, 2 * k)
@@ -443,15 +455,15 @@
     whole(line_tiles, pw_sem.at[2], pw_sem.at[3]).wait_send()
 
     def drain_home(c, carry):
-        whole(hsend.at[c, z_others], hsend_sem.at[c], home_sem.at[c, 0]).wait_send()
+        whole(hsend.at[c, z_others], hsend_sem.at[c], home_sem.at[c]).wait_send()
         return carry
 
     lax.fori_loop(0, last, drain_home, 0)
-    whole(home.at[last, z_half_others], hsend_sem.at[last], home_sem.at[last, 0]).wait_recv()
+    whole(home.at[last, z_half_others], hsend_sem.at[last], home_sem.at[last]).wait_recv()
     for xp in range(some):
         add_up(last, home.at[last], 0, xp, 2 * xp)
     drain_home(last, 0)
-    whole(home.at[last, z_half_others], hsend_sem.at[last], home_sem.at[last, 1]).wait_recv()
+    whole(home.at[last, z_half_others], hsend_sem.at[last], home_sem.at[last + 1]).wait_recv()
 
 
 def finish_kernel(dims, acc, home, back, out_ref, stage, out_sem):
@@ -552,7 +564,7 @@
             dma((chunks,)),
             dma((chunks,)),
             dma((chunks,)),
-            dma((chunks, 2)),
+            dma((chunks + 1,)),
             dma((4,)),
         ],
         compiler_params=pltpu.CompilerParams(

time: 190 us -> 188 us (0.989)
  Pallas kernels: 190 us -> 188 us
where the time goes in v3:
time: 188 us
  Pallas kernels  188 us (100%)
    pallas_call x1, Pallas kernels, in_kernels(): pl.pallas_call(functools.partial(step_kernel, dims), out_shape=(jax.Shape...  186 us

profile of v3, /device:TPU:0, one launch (start us, length us, event | category | flops | bytes accessed | tf_op | source)
XLA Modules:
  0.0 188.1 jit_solution(14393580962985416173)
XLA Ops:
  0.0 0.0 copy-start
  0.0 186.0 %shard_map.64 = (f32[2,16,256,128]{3,2,1,0:T(8,128)S(1)}, f32[8,1024,128]{2,1,0:T(8,128)S(1)}) custom-call(f32[2,16,256,128]{3,2,1,0:T(8,128)} %field_ref.1, bf16[8,128,512]{2,1,0:T(8,128)(2,1)} %constant.10.clone.fwd_ref, bf16[512,256]{1,0:T(8,128)(2,1)} %constant.11.clone.across_ref, bf16[2,2,512,512]{3,2,1,0:T(8,128)(2,1)} %constant.12.clone.time_ref, ...), custom_call_target="tpu_custom_call" | custom-call | tf_op jit(solution)/shard_map/pallas_call | solution.py:530
  186.0 0.0 copy-done
  186.0 2.1 %shard_map.65 = f32[2,16,256,128]{3,2,1,0:T(8,128)} custom-call(f32[2,16,256,128]{3,2,1,0:T(8,128)S(1)} %get-tuple-element.7.acc, f32[8,1024,128]{2,1,0:T(8,128)S(1)} %get-tuple-element.8.home, bf16[512,192]{1,0:T(8,128)(2,1)S(1)} %copy-done), custom_call_target="tpu_custom_call" | custom-call | tf_op jit(solution)/shard_map/pallas_call | solution.py:574
Async XLA Ops:
  0.0 186.0 %copy-start = (bf16[512,192]{1,0:T(8,128)(2,1)S(1)}, bf16[512,192]{1,0:T(8,128)(2,1)}, u32[]{:S(2)}) copy-start(bf16[512,192]{1,0:T(8,128)(2,1)} %constant.14.clone.back) | copy-start | bytes 589828

commit v4 on v3

--- a/solution.py
+++ b/solution.py
@@ -139,6 +139,8 @@
     hsend_sem,
     home_sem,
     pw_sem,
+    line_ready,
+    ring_ready,
 ):
     slabs, times, rows, ny, cols, chunks = dims
     group = slabs * times
@@ -182,10 +184,48 @@
     ring = [(s + k) % slabs for k in range(1, slabs)]
 
     barrier = pltpu.get_barrier_semaphore()
-    for there in line:
-        pl.semaphore_signal(barrier, inc=1, device_id=(s, there), device_id_type=MESH)
-    for there in ring:
-        pl.semaphore_signal(barrier, inc=1, device_id=(there, m), device_id_type=MESH)
+    for k in range(1, times):
+
+        @pl.when(m + k < times)
+        def _():
+            pl.semaphore_signal(barrier, inc=1, device_id=(s, m + k), device_id_type=MESH)
+
+    for k in range(1, slabs):
+
+        @pl.when(s + k < slabs)
+        def _():
+            pl.semaphore_signal(barrier, inc=1, device_id=(s + k, m), device_id_type=MESH)
+
+    def answer():
+        @pl.when(m + s > 0)
+        def _():
+            pl.semaphore_wait(barrier, m + s)
+
+        for k in range(1, times):
+
+            @pl.when(m >= k)
+            def _():
+                pl.semaphore_signal(
+                    line_ready.at[m], inc=1, device_id=(s, m - k), device_id_type=MESH
+                )
+
+        for k in range(1, slabs):
+
+            @pl.when(s >= k)
+            def _():
+                pl.semaphore_signal(
+                    ring_ready.at[s], inc=1, device_id=(s - k, m), device_id_type=MESH
+                )
+
+    def await_line(there):
+        @pl.when(there > m)
+        def _():
+            pl.semaphore_wait(line_ready.at[there], 1)
+
+    def await_ring(there):
+        @pl.when(there > s)
+        def _():
+            pl.semaphore_wait(ring_ready.at[there], 1)
 
     def remote(src, dst, first, second, device):
         return pltpu.make_async_remote_copy(
@@ -200,8 +240,8 @@
     def whole(ref, first, second):
         return remote(ref, ref, first, second, (s, m))
 
-    def out_along_t(c, first, count):
-        for there in line:
+    def out_along_t(c, first, count, peers):
+        for there in peers:
             remote(
                 zsend.at[c, pl.ds(there * zblk + first, count)],
                 zrecv.at[c, pl.ds(m * zblk + first, count)],
@@ -275,6 +315,7 @@
             if xp < some:
                 field_copy(some + xp).start()
         if h == 0:
+            answer()
             tables[0].wait()
         else:
             for copy in tables[1:]:
@@ -282,16 +323,20 @@
             tile = jnp.sum(total[:, :cols] + total[:, cols:], axis=0, keepdims=True)
             pw_send[0] = tile
             pw_recv[s] = tile
-            for there in ring:
-                remote(
-                    pw_send.at[0], pw_recv.at[s], pw_sem.at[0], pw_sem.at[1], (there, m)
-                ).start()
         for xp in range(h * some, (h + 1) * some):
             along_y(0, xp)
         lay_out(0, h)
         if h == 0:
-            pl.semaphore_wait(barrier, times - 1 + slabs - 1)
-        out_along_t(0, h * zhalf, zhalf)
+            await_line(line[0])
+            out_along_t(0, 0, zhalf, line[:1])
+        else:
+            for there in line[1:]:
+                await_line(there)
+            out_along_t(0, 0, zhalf, line[1:])
+            out_along_t(0, zhalf, zhalf, line)
+    for there in ring:
+        await_ring(there)
+        remote(pw_send.at[0], pw_recv.at[s], pw_sem.at[0], pw_sem.at[1], (there, m)).start()
     slab_tiles = pw_recv.at[pl.ds(0, slabs - 1)]
     whole(slab_tiles, pw_sem.at[0], pw_sem.at[1]).wait_recv()
     tile = jnp.sum(pw_recv[...], axis=0)
@@ -309,7 +354,7 @@
         lax.fori_loop(0, pairs, body, 0)
         for h in range(2):
             lay_out(c, h)
-        out_along_t(c, 0, zblk)
+        out_along_t(c, 0, zblk, line)
         return carry
 
     lax.fori_loop(1, chunks, rest, 0)
@@ -566,6 +611,8 @@
             dma((chunks,)),
             dma((chunks + 1,)),
             dma((4,)),
+            pltpu.SemaphoreType.REGULAR((times,)),
+            pltpu.SemaphoreType.REGULAR((slabs,)),
         ],
         compiler_params=pltpu.CompilerParams(
             collective_id=0, has_side_effects=True, vmem_limit_bytes=45 * 1024 * 1024

time: 188 us -> 188 us (level)
  no operation moved by 1% of the time
where the time goes in v4:
time: 188 us
  Pallas kernels  188 us (100%)
    pallas_call x1, Pallas kernels, in_kernels(): pl.pallas_call(functools.partial(step_kernel, dims), out_shape=(jax.Shape...  186 us

profile of v4, /device:TPU:0, one launch (start us, length us, event | category | flops | bytes accessed | tf_op | source)
XLA Modules:
  0.0 187.8 jit_solution(1713146988266633844)
XLA Ops:
  0.0 0.0 copy-start
  0.0 185.7 %shard_map.64 = (f32[2,16,256,128]{3,2,1,0:T(8,128)S(1)}, f32[8,1024,128]{2,1,0:T(8,128)S(1)}) custom-call(f32[2,16,256,128]{3,2,1,0:T(8,128)} %field_ref.1, bf16[8,128,512]{2,1,0:T(8,128)(2,1)} %constant.10.clone.fwd_ref, bf16[512,256]{1,0:T(8,128)(2,1)} %constant.11.clone.across_ref, bf16[2,2,512,512]{3,2,1,0:T(8,128)(2,1)} %constant.12.clone.time_ref, ...), custom_call_target="tpu_custom_call" | custom-call | tf_op jit(solution)/shard_map/pallas_call | solution.py:575
  185.7 0.0 copy-done
  185.7 2.1 %shard_map.65 = f32[2,16,256,128]{3,2,1,0:T(8,128)} custom-call(f32[2,16,256,128]{3,2,1,0:T(8,128)S(1)} %get-tuple-element.7.acc, f32[8,1024,128]{2,1,0:T(8,128)S(1)} %get-tuple-element.8.home, bf16[512,192]{1,0:T(8,128)(2,1)S(1)} %copy-done), custom_call_target="tpu_custom_call" | custom-call | tf_op jit(solution)/shard_map/pallas_call | solution.py:621
Async XLA Ops:
  0.0 185.7 %copy-start = (bf16[512,192]{1,0:T(8,128)(2,1)S(1)}, bf16[512,192]{1,0:T(8,128)(2,1)}, u32[]{:S(2)}) copy-start(bf16[512,192]{1,0:T(8,128)(2,1)} %constant.14.clone.back) | copy-start | bytes 589828

commit v5 on v3

--- a/solution.py
+++ b/solution.py
@@ -200,8 +200,8 @@
     def whole(ref, first, second):
         return remote(ref, ref, first, second, (s, m))
 
-    def out_along_t(c, first, count):
-        for there in line:
+    def out_along_t(c, first, count, peers):
+        for there in peers:
             remote(
                 zsend.at[c, pl.ds(there * zblk + first, count)],
                 zrecv.at[c, pl.ds(m * zblk + first, count)],
@@ -291,7 +291,19 @@
         lay_out(0, h)
         if h == 0:
             pl.semaphore_wait(barrier, times - 1 + slabs - 1)
-        out_along_t(0, h * zhalf, zhalf)
+        if h == 0:
+            out_along_t(0, 0, zhalf, line[:1])
+
+            @pl.when(s % 2 == 0)
+            def _():
+                out_along_t(0, 0, zhalf, line[1:])
+        else:
+
+            @pl.when(s % 2 == 1)
+            def _():
+                out_along_t(0, 0, zhalf, line[1:])
+
+            out_along_t(0, zhalf, zhalf, line)
     slab_tiles = pw_recv.at[pl.ds(0, slabs - 1)]
     whole(slab_tiles, pw_sem.at[0], pw_sem.at[1]).wait_recv()
     tile = jnp.sum(pw_recv[...], axis=0)
@@ -309,7 +321,7 @@
         lax.fori_loop(0, pairs, body, 0)
         for h in range(2):
             lay_out(c, h)
-        out_along_t(c, 0, zblk)
+        out_along_t(c, 0, zblk, line)
         return carry
 
     lax.fori_loop(1, chunks, rest, 0)

time: 188 us -> 188 us (level)
  no operation moved by 1% of the time
where the time goes in v5:
time: 188 us
  Pallas kernels  188 us (100%)
    pallas_call x1, Pallas kernels, in_kernels(): pl.pallas_call(functools.partial(step_kernel, dims), out_shape=(jax.Shape...  186 us

profile of v5, /device:TPU:0, one launch (start us, length us, event | category | flops | bytes accessed | tf_op | source)
XLA Modules:
  0.0 188.1 jit_solution(18257849279445003500)
XLA Ops:
  0.0 0.0 copy-start
  0.0 185.9 %shard_map.64 = (f32[2,16,256,128]{3,2,1,0:T(8,128)S(1)}, f32[8,1024,128]{2,1,0:T(8,128)S(1)}) custom-call(f32[2,16,256,128]{3,2,1,0:T(8,128)} %field_ref.1, bf16[8,128,512]{2,1,0:T(8,128)(2,1)} %constant.10.clone.fwd_ref, bf16[512,256]{1,0:T(8,128)(2,1)} %constant.11.clone.across_ref, bf16[2,2,512,512]{3,2,1,0:T(8,128)(2,1)} %constant.12.clone.time_ref, ...), custom_call_target="tpu_custom_call" | custom-call | tf_op jit(solution)/shard_map/pallas_call | solution.py:542
  186.0 0.0 copy-done
  186.0 2.1 %shard_map.65 = f32[2,16,256,128]{3,2,1,0:T(8,128)} custom-call(f32[2,16,256,128]{3,2,1,0:T(8,128)S(1)} %get-tuple-element.7.acc, f32[8,1024,128]{2,1,0:T(8,128)S(1)} %get-tuple-element.8.home, bf16[512,192]{1,0:T(8,128)(2,1)S(1)} %copy-done), custom_call_target="tpu_custom_call" | custom-call | tf_op jit(solution)/shard_map/pallas_call | solution.py:586
Async XLA Ops:
  0.0 186.0 %copy-start = (bf16[512,192]{1,0:T(8,128)(2,1)S(1)}, bf16[512,192]{1,0:T(8,128)(2,1)}, u32[]{:S(2)}) copy-start(bf16[512,192]{1,0:T(8,128)(2,1)} %constant.14.clone.back) | copy-start | bytes 589828
